TPU v7x, 32 devices: a whole 2x2x4 slice. The times are simulated.
32 devices in a mesh: gx: 4 (over y, x), gy: 8 (over z, core).
Axes of the slice: x: 2, y: 2, z: 4, core: 2. Of those that a mesh axis runs over, the one named last changes fastest.
Arguments:
- velocity: float32 [3, 128, 64, 128], P(None, 'gx', 'gy'), may hold values from -6 to 6
- stress: float32 [6, 128, 64, 128], P(None, 'gx', 'gy'), may hold values from -6 to 6
- lame_first: float32 [128, 64, 128], P('gx', 'gy'), may hold values from 0.5 to 2
- modulus: float32 [128, 64, 128], P('gx', 'gy'), may hold values from 0.5 to 2
- buoyancy: float32 [128, 64, 128], P('gx', 'gy'), may hold values from 0.5 to 2
- zone: int32 [128, 64, 128], P('gx', 'gy'), may hold values from 0 to 7
- eligible: int32 [128, 64, 128], P('gx', 'gy'), may hold values 0 or 1
- cohesion: float32 [8], replicated, may hold values from 0.2 to 2
- friction: float32 [8], replicated, may hold values from 0.1 to 0.6
- source_cell: int32 [16], replicated, may hold values from 0 to 1048575
- source_moment: float32 [6, 16], replicated, may hold values from -15 to 15
Outputs:
- velocity_out: float32 [3, 128, 64, 128], P(None, 'gx', 'gy')
- stress_out: float32 [6, 128, 64, 128], P(None, 'gx', 'gy')
All inputs are finite; a program needn't handle non-finite values. No bound on the sum of `eligible` on one device may be relied on, other than what follows from the above.
Results may differ from a plain program's by a relative error of at most 0.00011.
Values sent between devices are 32-bit elements; how exact they have to be, the bound alone decides.
A program may use at most 64 MiB of HBM per device.

v0:
```python
import jax
import jax.numpy as jnp
from jax import lax
from jax.sharding import PartitionSpec as P

STEPS = 2


time_step = 0.1
near_weight = 9.0 / 8.0
far_weight = 1.0 / 24.0
shear_floor = 0.25


def extended(block, sides, width):
    for axis, dim in sides:
        count = lax.axis_size(axis)
        forward = [(i, i + 1) for i in range(count - 1)]
        backward = [(target, source) for source, target in forward]
        low = lax.ppermute(
            lax.slice_in_dim(block, block.shape[dim] - width, None, axis=dim), axis, forward
        )
        high = lax.ppermute(lax.slice_in_dim(block, 0, width, axis=dim), axis, backward)
        block = jnp.concatenate([low, block, high], axis=dim)
    return block


def crop(padded, axis, offset):
    result = padded
    for dim in range(3):
        begin = offset if dim == axis else 2
        length = padded.shape[dim] - 4
        result = lax.slice_in_dim(result, begin, begin + length, axis=dim)
    return result


def derivative(padded, axis, forward):
    if forward:
        return near_weight * (crop(padded, axis, 3) - crop(padded, axis, 2)) - far_weight * (
            crop(padded, axis, 4) - crop(padded, axis, 1)
        )
    return near_weight * (crop(padded, axis, 2) - crop(padded, axis, 1)) - far_weight * (
        crop(padded, axis, 3) - crop(padded, axis, 0)
    )


def split_velocity_update(along_x, along_y, along_z, velocity, buoyancy):
    force_x = (
        derivative(along_x[0], 0, True)
        + derivative(along_y[0], 1, False)
        + derivative(along_z[0], 2, False)
    )
    force_y = (
        derivative(along_x[1], 0, False)
        + derivative(along_y[1], 1, True)
        + derivative(along_z[1], 2, False)
    )
    force_z = (
        derivative(along_x[2], 0, False)
        + derivative(along_y[2], 1, False)
        + derivative(along_z[2], 2, True)
    )
    forces = jnp.stack([force_x, force_y, force_z])
    return velocity + time_step * buoyancy[None] * forces


def stress_update(flow_pad, stress, lame_first, modulus):
    strain_x = derivative(flow_pad[0], 0, False)
    strain_y = derivative(flow_pad[1], 1, False)
    strain_z = derivative(flow_pad[2], 2, False)
    dilation = strain_x + strain_y + strain_z
    shear_xy = derivative(flow_pad[0], 1, True) + derivative(flow_pad[1], 0, True)
    shear_xz = derivative(flow_pad[0], 2, True) + derivative(flow_pad[2], 0, True)
    shear_yz = derivative(flow_pad[1], 2, True) + derivative(flow_pad[2], 1, True)
    rates = jnp.stack(
        [
            lame_first * dilation + 2.0 * modulus * strain_x,
            lame_first * dilation + 2.0 * modulus * strain_y,
            lame_first * dilation + 2.0 * modulus * strain_z,
            modulus * shear_xy,
            modulus * shear_xz,
            modulus * shear_yz,
        ]
    )
    return stress + time_step * rates


def plastic(stress, cell_cohesion, cell_friction, eligible):
    pressure = (stress[0] + stress[1] + stress[2]) / 3.0
    dev_x = stress[0] - pressure
    dev_y = stress[1] - pressure
    dev_z = stress[2] - pressure
    second = (
        0.5 * (dev_x * dev_x + dev_y * dev_y + dev_z * dev_z)
        + stress[3] * stress[3]
        + stress[4] * stress[4]
        + stress[5] * stress[5]
    )
    strength = jnp.maximum(
        cell_cohesion * jnp.sqrt(1.0 - cell_friction * cell_friction) - pressure * cell_friction,
        0.0,
    )
    ratio = jnp.minimum(1.0, strength / jnp.maximum(jnp.sqrt(second), shear_floor))
    factor = jnp.where(eligible == 1, ratio, 1.0)
    return jnp.stack(
        [
            pressure + factor * dev_x,
            pressure + factor * dev_y,
            pressure + factor * dev_z,
            factor * stress[3],
            factor * stress[4],
            factor * stress[5],
        ]
    )


def pad_depth(field, width):
    return jnp.pad(field, ((0, 0), (0, 0), (0, 0), (width, width)))


def on_device(
    velocity,
    stress,
    lame_first,
    modulus,
    buoyancy,
    zone,
    eligible,
    cohesion,
    friction,
    source_cell,
    source_moment,
):
    rows_x, rows_y, depth = zone.shape
    total_y = rows_y * lax.axis_size("gy")
    start_x = lax.axis_index("gx") * rows_x
    start_y = lax.axis_index("gy") * rows_y
    cell_cohesion = jnp.zeros(zone.shape, jnp.float32)
    cell_friction = jnp.zeros(zone.shape, jnp.float32)
    for which in range(cohesion.shape[0]):
        hit = zone == which
        cell_cohesion = cell_cohesion + jnp.where(hit, cohesion[which], 0.0)
        cell_friction = cell_friction + jnp.where(hit, friction[which], 0.0)
    plane = total_y * depth
    src_x = source_cell // plane
    src_y = source_cell // depth % total_y
    src_z = source_cell % depth
    pick_x = (src_x[:, None] == start_x + jnp.arange(rows_x, dtype=jnp.int32)[None]).astype(
        jnp.float32
    )
    pick_y = (src_y[:, None] == start_y + jnp.arange(rows_y, dtype=jnp.int32)[None]).astype(
        jnp.float32
    )
    pick_z = (src_z[:, None] == jnp.arange(depth, dtype=jnp.int32)[None]).astype(jnp.float32)
    injection = jnp.einsum(
        "cs,sx,sy,sz->cxyz",
        time_step * source_moment,
        pick_x,
        pick_y,
        pick_z,
        precision=lax.Precision.HIGHEST,
    )
    for step in range(STEPS):
        strike_part = jnp.stack([stress[0], stress[3], stress[4]])
        normal_part = jnp.stack([stress[3], stress[1], stress[5]])
        depth_part = jnp.stack([stress[4], stress[5], stress[2]])
        along_x = extended(strike_part, (("gx", 1),), 2)
        along_y = extended(normal_part, (("gy", 2),), 2)
        along_x = jnp.pad(along_x, ((0, 0), (0, 0), (2, 2), (2, 2)))
        along_y = jnp.pad(along_y, ((0, 0), (2, 2), (0, 0), (2, 2)))
        along_z = jnp.pad(depth_part, ((0, 0), (2, 2), (2, 2), (2, 2)))
        velocity = split_velocity_update(along_x, along_y, along_z, velocity, buoyancy)
        flow_pad = extended(velocity, (("gx", 1), ("gy", 2)), 2)
        stress = stress_update(pad_depth(flow_pad, 2), stress, lame_first, modulus)
        stress = stress + injection
        stress = plastic(stress, cell_cohesion, cell_friction, eligible)
    return (velocity, stress)


def solution(mesh):
    placed = (
        P(None, "gx", "gy", None),
        P(None, "gx", "gy", None),
        P("gx", "gy", None),
        P("gx", "gy", None),
        P("gx", "gy", None),
        P("gx", "gy", None),
        P("gx", "gy", None),
        P(),
        P(),
        P(),
        P(),
    )
    return jax.shard_map(
        on_device,
        mesh=mesh,
        in_specs=placed,
        out_specs=(P(None, "gx", "gy", None), P(None, "gx", "gy", None)),
        check_vma=False,
    )
```

profile of v0, /device:TPU:1, one launch (start us, length us, event | category | flops | bytes accessed | tf_op | source)
XLA Modules:
  0.0 108.4 jit_solution(15015662236129044478)
XLA Ops:
  0.6 1.1 %fusion.184 = (f32[2,32,8,128]{3,2,1,0:T(8,128)S(1)}, f32[2,32,8,128]{3,2,1,0:T(8,128)S(1)}) fusion(f32[6,32,8,128]{3,2,1,0:T(8,128)} %param.12), kind=kLoop, calls=%fused_computation.440 | loop fusion | bytes 1048576 | tf_op jit(solution)/shard_map/slice | solution.py:164
  2.1 3.9 %collective-permute-start = (f32[3,2,8,128]{3,1,2,0:T(2,128)S(1)}, f32[3,2,8,128]{3,1,2,0:T(2,128)S(1)}, u32[]{:S(2)}, u32[]{:S(2)}) collective-permute-start(f32[3,2,8,128]{3,1,2,0:T(2,128)S(1)} %get-tuple-element.117), channel_id=1, source_target_pairs={{0,8},{8,16},{16,24},{1,9},{9,17},{17,25},{2,10},{10,18},{18,26},{... | collective-permute-start | bytes 73736 | tf_op jit(solution)/shard_map/ppermute | solution.py:20
  6.1 1.3 %collective-permute-start.1 = (f32[3,2,8,128]{3,1,2,0:T(2,128)S(1)}, f32[3,2,8,128]{3,1,2,0:T(2,128)S(1)}, u32[]{:S(2)}, u32[]{:S(2)}) collective-permute-start(f32[3,2,8,128]{3,1,2,0:T(2,128)S(1)} %get-tuple-element.118), channel_id=1, source_target_pairs={{8,0},{16,8},{24,16},{9,1},{17,9},{25,17},{10,2},{18,10},{26,18},{... | collective-permute-start | bytes 73736 | tf_op jit(solution)/shard_map/ppermute | solution.py:23
  7.5 4.0 %collective-permute-start.2 = (f32[3,32,2,128]{3,1,2,0:T(8,128)S(1)}, f32[3,32,2,128]{3,1,2,0:T(8,128)S(1)}, u32[]{:S(2)}, u32[]{:S(2)}) collective-permute-start(f32[3,32,2,128]{3,1,2,0:T(8,128)S(1)} %get-tuple-element.119), channel_id=1, source_target_pairs={{0,1},{1,2},{2,3},{3,4},{4,5},{5,6},{6,7},{8,9},{9,10},{10,11},{11... | collective-permute-start | bytes 294920 | tf_op jit(solution)/shard_map/ppermute | solution.py:20
  11.5 1.9 %collective-permute-start.3 = (f32[3,32,2,128]{3,1,2,0:T(8,128)S(1)}, f32[3,32,2,128]{3,1,2,0:T(8,128)S(1)}, u32[]{:S(2)}, u32[]{:S(2)}) collective-permute-start(f32[3,32,2,128]{3,1,2,0:T(8,128)S(1)} %get-tuple-element.120), channel_id=1, source_target_pairs={{1,0},{2,1},{3,2},{4,3},{5,4},{6,5},{7,6},{9,8},{10,9},{11,10},{12... | collective-permute-start | bytes 294920 | tf_op jit(solution)/shard_map/ppermute | solution.py:23
  14.4 1.0 convolution_bitcast_fusion
  15.4 0.5 select_maximum_fusion.23
  15.9 0.6 slice_bitcast_fusion.59
  16.5 0.9 collective-permute-done.3
  17.5 0.5 select_maximum_fusion.19
  18.1 0.4 fusion.142
  18.5 0.4 fusion.154
  19.0 0.5 fusion.130
  19.7 4.3 %collective-permute-start.4 = (f32[3,2,8,128]{3,1,2,0:T(2,128)S(1)}, f32[3,2,8,128]{3,1,2,0:T(2,128)S(1)}, u32[]{:S(2)}, u32[]{:S(2)}) collective-permute-start(f32[3,2,8,128]{3,1,2,0:T(2,128)S(1)} %get-tuple-element.115), channel_id=1, source_target_pairs={{0,8},{8,16},{16,24},{1,9},{9,17},{17,25},{2,10},{10,18},{18,26},{... | collective-permute-start | bytes 73736 | tf_op jit(solution)/shard_map/ppermute | solution.py:20
  24.0 1.3 %collective-permute-start.5 = (f32[3,2,8,128]{3,1,2,0:T(2,128)S(1)}, f32[3,2,8,128]{3,1,2,0:T(2,128)S(1)}, u32[]{:S(2)}, u32[]{:S(2)}) collective-permute-start(f32[3,2,8,128]{3,1,2,0:T(2,128)S(1)} %get-tuple-element.116), channel_id=1, source_target_pairs={{8,0},{16,8},{24,16},{9,1},{17,9},{25,17},{10,2},{18,10},{26,18},{... | collective-permute-start | bytes 73736 | tf_op jit(solution)/shard_map/ppermute | solution.py:23
  25.3 0.7 fusion.187
  25.9 3.3 %collective-permute-done.5 = f32[3,2,8,128]{3,1,2,0:T(2,128)S(1)} collective-permute-done((f32[3,2,8,128]{3,1,2,0:T(2,128)S(1)}, f32[3,2,8,128]{3,1,2,0:T(2,128)S(1)}, u32[]{:S(2)}, u32[]{:S(2)}) %collective-permute-start.5) | collective-permute-done | bytes 24608 | tf_op jit(solution)/shard_map/ppermute | solution.py:23
  29.2 4.0 %collective-permute-start.6 = (f32[3,36,2,128]{3,1,2,0:T(8,128)S(1)}, f32[3,36,2,128]{3,1,2,0:T(8,128)S(1)}, u32[]{:S(2)}, u32[]{:S(2)}) collective-permute-start(f32[3,36,2,128]{3,1,2,0:T(8,128)S(1)} %get-tuple-element.107), channel_id=1, source_target_pairs={{0,1},{1,2},{2,3},{3,4},{4,5},{5,6},{6,7},{8,9},{9,10},{10,11},{11... | collective-permute-start | bytes 331784 | tf_op jit(solution)/shard_map/ppermute | solution.py:20
  33.3 1.9 %collective-permute-start.7 = (f32[3,36,2,128]{3,1,2,0:T(8,128)S(1)}, f32[3,36,2,128]{3,1,2,0:T(8,128)S(1)}, u32[]{:S(2)}, u32[]{:S(2)}) collective-permute-start(f32[3,36,2,128]{3,1,2,0:T(8,128)S(1)} %get-tuple-element.108), channel_id=1, source_target_pairs={{1,0},{2,1},{3,2},{4,3},{5,4},{6,5},{7,6},{9,8},{10,9},{11,10},{12... | collective-permute-start | bytes 331784 | tf_op jit(solution)/shard_map/ppermute | solution.py:23
  35.2 0.7 fusion.188
  35.9 3.6 %collective-permute-done.7 = f32[3,36,2,128]{3,1,2,0:T(8,128)S(1)} collective-permute-done((f32[3,36,2,128]{3,1,2,0:T(8,128)S(1)}, f32[3,36,2,128]{3,1,2,0:T(8,128)S(1)}, u32[]{:S(2)}, u32[]{:S(2)}) %collective-permute-start.7) | collective-permute-done | bytes 110624 | tf_op jit(solution)/shard_map/ppermute | solution.py:23
  39.5 0.6 select_maximum_fusion.14
  40.1 0.6 slice_bitcast_fusion.32
  41.0 0.4 bitcast_dynamic-update-slice_fusion.11
  42.9 0.6 copy-done.4
  43.6 10.6 %constant_dynamic-update-slice_fusion.5 = (f32[6,32,8,128]{3,1,2,0:T(8,128)S(1)}, f32[1,32,8,128]{3,1,2,0:T(8,128)S(1)}, f32[32,8,128]{2,0,1:T(8,128)S(1)}, pred...) fusion(f32[6,32,8,128]{3,1,2,0:T(8,128)S(1)} %copy_add_fusion.1, ...), kind=kLoop, calls=%fused_computation.407 | loop fusion | flops 2260991 | bytes 1867840
  54.3 1.9 %collective-permute-start.10 = (f32[3,32,2,128]{3,1,2,0:T(8,128)S(1)}, f32[3,32,2,128]{3,1,2,0:T(8,128)S(1)}, u32[]{:S(2)}, u32[]{:S(2)}) collective-permute-start(f32[3,32,2,128]{3,1,2,0:T(8,128)S(1)} %get-tuple-element.113), channel_id=1, source_target_pairs={{0,1},{1,2},{2,3},{3,4},{4,5},{5,6},{6,7},{8,9},{9,10},{10,11},{11... | collective-permute-start | bytes 294920 | tf_op jit(solution)/shard_map/ppermute | solution.py:20
  56.3 2.4 %collective-permute-start.11 = (f32[3,32,2,128]{3,1,2,0:T(8,128)S(1)}, f32[3,32,2,128]{3,1,2,0:T(8,128)S(1)}, u32[]{:S(2)}, u32[]{:S(2)}) collective-permute-start(f32[3,32,2,128]{3,1,2,0:T(8,128)S(1)} %get-tuple-element.114), channel_id=1, source_target_pairs={{1,0},{2,1},{3,2},{4,3},{5,4},{6,5},{7,6},{9,8},{10,9},{11,10},{12... | collective-permute-start | bytes 294920 | tf_op jit(solution)/shard_map/ppermute | solution.py:23
  58.7 4.4 %collective-permute-start.8 = (f32[3,2,8,128]{3,1,2,0:T(2,128)S(1)}, f32[3,2,8,128]{3,1,2,0:T(2,128)S(1)}, u32[]{:S(2)}, u32[]{:S(2)}) collective-permute-start(f32[3,2,8,128]{3,1,2,0:T(2,128)S(1)} %get-tuple-element.111), channel_id=1, source_target_pairs={{0,8},{8,16},{16,24},{1,9},{9,17},{17,25},{2,10},{10,18},{18,26},{... | collective-permute-start | bytes 73736 | tf_op jit(solution)/shard_map/ppermute | solution.py:20
  63.1 1.5 %collective-permute-start.9 = (f32[3,2,8,128]{3,1,2,0:T(2,128)S(1)}, f32[3,2,8,128]{3,1,2,0:T(2,128)S(1)}, u32[]{:S(2)}, u32[]{:S(2)}) collective-permute-start(f32[3,2,8,128]{3,1,2,0:T(2,128)S(1)} %get-tuple-element.112), channel_id=1, source_target_pairs={{8,0},{16,8},{24,16},{9,1},{17,9},{25,17},{10,2},{18,10},{26,18},{... | collective-permute-start | bytes 73736 | tf_op jit(solution)/shard_map/ppermute | solution.py:23
  64.6 3.5 %collective-permute-done.9 = f32[3,2,8,128]{3,1,2,0:T(2,128)S(1)} collective-permute-done((f32[3,2,8,128]{3,1,2,0:T(2,128)S(1)}, f32[3,2,8,128]{3,1,2,0:T(2,128)S(1)}, u32[]{:S(2)}, u32[]{:S(2)}) %collective-permute-start.9) | collective-permute-done | bytes 24608 | tf_op jit(solution)/shard_map/ppermute | solution.py:23
  68.1 3.8 %select_maximum_fusion.10 = (f32[3,36,12,132]{3,1,2,0:T(8,128)S(1)}, f32[3,36,12,132]{3,1,2,0:T(8,128)S(1)}, f32[3,36,12,132]{3,1,2,0:T(8,128)S(1)}) fusion(f32[3,2,8,128]{3,1,2,0:T(2,128)S(1)} %collective-permute-done.9, f32[3,2,8,128]{3,1,2,0:T(2,128)S(1)} %collective-permute-done.8, f32[1,32,8,128]{3,1,2,0:T(8,128)S(1)} %get-tuple-element.14, ...), kind=kLoop, calls=%fused_computation.26 | loop fusion | flops 9408960 | bytes 3085056 | tf_op jit(solution)/shard_map/concatenate | solution.py:24
  71.9 0.6 slice_bitcast_fusion.29
  72.9 0.5 fusion.67
  73.3 0.4 fusion.79
  73.8 0.5 fusion.55
  74.4 2.6 %collective-permute-start.12 = (f32[3,2,8,128]{3,1,2,0:T(2,128)S(1)}, f32[3,2,8,128]{3,1,2,0:T(2,128)S(1)}, u32[]{:S(2)}, u32[]{:S(2)}) collective-permute-start(f32[3,2,8,128]{3,1,2,0:T(2,128)S(1)} %get-tuple-element.109), channel_id=1, source_target_pairs={{0,8},{8,16},{16,24},{1,9},{9,17},{17,25},{2,10},{10,18},{18,26},{... | collective-permute-start | bytes 73736 | tf_op jit(solution)/shard_map/ppermute | solution.py:20
  77.1 1.3 %collective-permute-start.13 = (f32[3,2,8,128]{3,1,2,0:T(2,128)S(1)}, f32[3,2,8,128]{3,1,2,0:T(2,128)S(1)}, u32[]{:S(2)}, u32[]{:S(2)}) collective-permute-start(f32[3,2,8,128]{3,1,2,0:T(2,128)S(1)} %get-tuple-element.110), channel_id=1, source_target_pairs={{8,0},{16,8},{24,16},{9,1},{17,9},{25,17},{10,2},{18,10},{26,18},{... | collective-permute-start | bytes 73736 | tf_op jit(solution)/shard_map/ppermute | solution.py:23
  78.4 3.3 %collective-permute-done.13 = f32[3,2,8,128]{3,1,2,0:T(2,128)S(1)} collective-permute-done((f32[3,2,8,128]{3,1,2,0:T(2,128)S(1)}, f32[3,2,8,128]{3,1,2,0:T(2,128)S(1)}, u32[]{:S(2)}, u32[]{:S(2)}) %collective-permute-start.13) | collective-permute-done | bytes 24608 | tf_op jit(solution)/shard_map/ppermute | solution.py:23
  81.7 5.5 %collective-permute-start.14 = (f32[3,36,2,128]{3,1,2,0:T(8,128)S(1)}, f32[3,36,2,128]{3,1,2,0:T(8,128)S(1)}, u32[]{:S(2)}, u32[]{:S(2)}) collective-permute-start(f32[3,36,2,128]{3,1,2,0:T(8,128)S(1)} %get-tuple-element.105), channel_id=1, source_target_pairs={{0,1},{1,2},{2,3},{3,4},{4,5},{5,6},{6,7},{8,9},{9,10},{10,11},{11... | collective-permute-start | bytes 331784 | tf_op jit(solution)/shard_map/ppermute | solution.py:20
  87.2 1.9 %collective-permute-start.15 = (f32[3,36,2,128]{3,1,2,0:T(8,128)S(1)}, f32[3,36,2,128]{3,1,2,0:T(8,128)S(1)}, u32[]{:S(2)}, u32[]{:S(2)}) collective-permute-start(f32[3,36,2,128]{3,1,2,0:T(8,128)S(1)} %get-tuple-element.106), channel_id=1, source_target_pairs={{1,0},{2,1},{3,2},{4,3},{5,4},{6,5},{7,6},{9,8},{10,9},{11,10},{12... | collective-permute-start | bytes 331784 | tf_op jit(solution)/shard_map/ppermute | solution.py:23
  89.1 1.0 copy.48
  90.1 3.3 %collective-permute-done.15 = f32[3,36,2,128]{3,1,2,0:T(8,128)S(1)} collective-permute-done((f32[3,36,2,128]{3,1,2,0:T(8,128)S(1)}, f32[3,36,2,128]{3,1,2,0:T(8,128)S(1)}, u32[]{:S(2)}, u32[]{:S(2)}) %collective-permute-start.15) | collective-permute-done | bytes 110624 | tf_op jit(solution)/shard_map/ppermute | solution.py:23
  93.4 0.6 select_maximum_fusion
  93.9 0.6 slice_bitcast_fusion.2
  94.6 0.4 bitcast_dynamic-update-slice_fusion.8
  96.4 10.5 %bitcast_dynamic-update-slice_fusion.5 = (f32[6,32,8,128]{3,1,2,0:T(8,128)S(1)}, f32[32,8,128]{2,0,1:T(8,128)S(1)}, f32[32,8,128]{2,0,1:T(8,128)S(1)}) fusion(f32[6,32,8,128]{3,1,0,2:T(8,128)S(1)} %copy_add_fusion, pred[32,8,128]{2,0,1:T(8,128)(4,1)S(1)} %get-tuple-element.32, pred[32,8,128]{2,0,1:T(8,128)(4,1)S(1)} %get-tuple-element.31, f32[]{:T(128)} %bitcast.62, ...), kind=kLoop, calls=%fused_computation.350 | loop fusion | flops 1966079 | bytes 1474624
  107.1 1.3 %copy.49 = f32[6,32,8,128]{3,2,1,0:T(8,128)} copy(f32[6,32,8,128]{3,1,2,0:T(8,128)S(1)} %bitcast_dynamic-update-slice_fusion) | data formatting | bytes 1572864
  (84 shorter events, 5.7 us)
Async XLA Ops:
  0.6 1.3 %copy-start.1 = (f32[6,32,8,128]{3,2,1,0:T(8,128)S(1)}, f32[6,32,8,128]{3,2,1,0:T(8,128)}, u32[]{:S(2)}) copy-start(f32[6,32,8,128]{3,2,1,0:T(8,128)} %param.12) | copy-start | bytes 2359300
  2.0 11.5 %copy-start.10 = (s32[16]{0:T(128)S(1)}, s32[16]{0:T(128)}, u32[]{:S(2)}) copy-start(s32[16]{0:T(128)} %param.20) | copy-start | bytes 196
  2.0 11.6 %copy-start.9 = (f32[6,16]{1,0:T(8,128)S(1)}, f32[6,16]{1,0:T(8,128)}, u32[]{:S(2)}) copy-start(f32[6,16]{1,0:T(8,128)} %param.21) | copy-start | bytes 1156
  2.1 13.3 %collective-permute-start = (f32[3,2,8,128]{3,1,2,0:T(2,128)S(1)}, f32[3,2,8,128]{3,1,2,0:T(2,128)S(1)}, u32[]{:S(2)}, u32[]{:S(2)}) collective-permute-start(f32[3,2,8,128]{3,1,2,0:T(2,128)S(1)} %get-tuple-element.117), channel_id=1, source_target_pairs={{0,8},{8,16},{16,24},{1,9},{9,17},{17,25},{2,10},{10,18},{18,26},{... | collective-permute-start | bytes 73736 | tf_op jit(solution)/shard_map/ppermute | solution.py:20
  6.1 9.4 %collective-permute-start.1 = (f32[3,2,8,128]{3,1,2,0:T(2,128)S(1)}, f32[3,2,8,128]{3,1,2,0:T(2,128)S(1)}, u32[]{:S(2)}, u32[]{:S(2)}) collective-permute-start(f32[3,2,8,128]{3,1,2,0:T(2,128)S(1)} %get-tuple-element.118), channel_id=1, source_target_pairs={{8,0},{16,8},{24,16},{9,1},{17,9},{25,17},{10,2},{18,10},{26,18},{... | collective-permute-start | bytes 73736 | tf_op jit(solution)/shard_map/ppermute | solution.py:23
  7.5 9.0 %collective-permute-start.2 = (f32[3,32,2,128]{3,1,2,0:T(8,128)S(1)}, f32[3,32,2,128]{3,1,2,0:T(8,128)S(1)}, u32[]{:S(2)}, u32[]{:S(2)}) collective-permute-start(f32[3,32,2,128]{3,1,2,0:T(8,128)S(1)} %get-tuple-element.119), channel_id=1, source_target_pairs={{0,1},{1,2},{2,3},{3,4},{4,5},{5,6},{6,7},{8,9},{9,10},{10,11},{11... | collective-permute-start | bytes 294920 | tf_op jit(solution)/shard_map/ppermute | solution.py:20
  11.5 5.9 %collective-permute-start.3 = (f32[3,32,2,128]{3,1,2,0:T(8,128)S(1)}, f32[3,32,2,128]{3,1,2,0:T(8,128)S(1)}, u32[]{:S(2)}, u32[]{:S(2)}) collective-permute-start(f32[3,32,2,128]{3,1,2,0:T(8,128)S(1)} %get-tuple-element.120), channel_id=1, source_target_pairs={{1,0},{2,1},{3,2},{4,3},{5,4},{6,5},{7,6},{9,8},{10,9},{11,10},{12... | collective-permute-start | bytes 294920 | tf_op jit(solution)/shard_map/ppermute | solution.py:23
  14.1 1.3 %copy-start.6 = (f32[32,8,128]{2,1,0:T(8,128)S(1)}, f32[32,8,128]{2,1,0:T(8,128)}, u32[]{:S(2)}) copy-start(f32[32,8,128]{2,1,0:T(8,128)} %param.15) | copy-start | bytes 393220
  18.5 1.0 copy-start.2
  19.0 6.3 %copy-start.7 = (f32[8]{0:T(128)S(1)}, f32[8]{0:T(128)}, u32[]{:S(2)}) copy-start(f32[8]{0:T(128)} %param.18) | copy-start | bytes 100
  19.5 15.7 %copy-start.8 = (f32[8]{0:T(128)S(1)}, f32[8]{0:T(128)}, u32[]{:S(2)}) copy-start(f32[8]{0:T(128)} %param.19) | copy-start | bytes 100
  19.7 6.3 %collective-permute-start.4 = (f32[3,2,8,128]{3,1,2,0:T(2,128)S(1)}, f32[3,2,8,128]{3,1,2,0:T(2,128)S(1)}, u32[]{:S(2)}, u32[]{:S(2)}) collective-permute-start(f32[3,2,8,128]{3,1,2,0:T(2,128)S(1)} %get-tuple-element.115), channel_id=1, source_target_pairs={{0,8},{8,16},{16,24},{1,9},{9,17},{17,25},{2,10},{10,18},{18,26},{... | collective-permute-start | bytes 73736 | tf_op jit(solution)/shard_map/ppermute | solution.py:20
  24.0 5.2 %collective-permute-start.5 = (f32[3,2,8,128]{3,1,2,0:T(2,128)S(1)}, f32[3,2,8,128]{3,1,2,0:T(2,128)S(1)}, u32[]{:S(2)}, u32[]{:S(2)}) collective-permute-start(f32[3,2,8,128]{3,1,2,0:T(2,128)S(1)} %get-tuple-element.116), channel_id=1, source_target_pairs={{8,0},{16,8},{24,16},{9,1},{17,9},{25,17},{10,2},{18,10},{26,18},{... | collective-permute-start | bytes 73736 | tf_op jit(solution)/shard_map/ppermute | solution.py:23
  29.2 6.7 %collective-permute-start.6 = (f32[3,36,2,128]{3,1,2,0:T(8,128)S(1)}, f32[3,36,2,128]{3,1,2,0:T(8,128)S(1)}, u32[]{:S(2)}, u32[]{:S(2)}) collective-permute-start(f32[3,36,2,128]{3,1,2,0:T(8,128)S(1)} %get-tuple-element.107), channel_id=1, source_target_pairs={{0,1},{1,2},{2,3},{3,4},{4,5},{5,6},{6,7},{8,9},{9,10},{10,11},{11... | collective-permute-start | bytes 331784 | tf_op jit(solution)/shard_map/ppermute | solution.py:20
  33.3 6.2 %collective-permute-start.7 = (f32[3,36,2,128]{3,1,2,0:T(8,128)S(1)}, f32[3,36,2,128]{3,1,2,0:T(8,128)S(1)}, u32[]{:S(2)}, u32[]{:S(2)}) collective-permute-start(f32[3,36,2,128]{3,1,2,0:T(8,128)S(1)} %get-tuple-element.108), channel_id=1, source_target_pairs={{1,0},{2,1},{3,2},{4,3},{5,4},{6,5},{7,6},{9,8},{10,9},{11,10},{12... | collective-permute-start | bytes 331784 | tf_op jit(solution)/shard_map/ppermute | solution.py:23
  40.0 0.9 copy-start
  40.0 1.0 copy-start.3
  42.6 0.9 copy-start.4
  42.6 1.0 copy-start.5
  54.3 13.7 %collective-permute-start.10 = (f32[3,32,2,128]{3,1,2,0:T(8,128)S(1)}, f32[3,32,2,128]{3,1,2,0:T(8,128)S(1)}, u32[]{:S(2)}, u32[]{:S(2)}) collective-permute-start(f32[3,32,2,128]{3,1,2,0:T(8,128)S(1)} %get-tuple-element.113), channel_id=1, source_target_pairs={{0,1},{1,2},{2,3},{3,4},{4,5},{5,6},{6,7},{8,9},{9,10},{10,11},{11... | collective-permute-start | bytes 294920 | tf_op jit(solution)/shard_map/ppermute | solution.py:20
  56.3 11.8 %collective-permute-start.11 = (f32[3,32,2,128]{3,1,2,0:T(8,128)S(1)}, f32[3,32,2,128]{3,1,2,0:T(8,128)S(1)}, u32[]{:S(2)}, u32[]{:S(2)}) collective-permute-start(f32[3,32,2,128]{3,1,2,0:T(8,128)S(1)} %get-tuple-element.114), channel_id=1, source_target_pairs={{1,0},{2,1},{3,2},{4,3},{5,4},{6,5},{7,6},{9,8},{10,9},{11,10},{12... | collective-permute-start | bytes 294920 | tf_op jit(solution)/shard_map/ppermute | solution.py:23
  58.7 5.9 %collective-permute-start.8 = (f32[3,2,8,128]{3,1,2,0:T(2,128)S(1)}, f32[3,2,8,128]{3,1,2,0:T(2,128)S(1)}, u32[]{:S(2)}, u32[]{:S(2)}) collective-permute-start(f32[3,2,8,128]{3,1,2,0:T(2,128)S(1)} %get-tuple-element.111), channel_id=1, source_target_pairs={{0,8},{8,16},{16,24},{1,9},{9,17},{17,25},{2,10},{10,18},{18,26},{... | collective-permute-start | bytes 73736 | tf_op jit(solution)/shard_map/ppermute | solution.py:20
  63.1 5.0 %collective-permute-start.9 = (f32[3,2,8,128]{3,1,2,0:T(2,128)S(1)}, f32[3,2,8,128]{3,1,2,0:T(2,128)S(1)}, u32[]{:S(2)}, u32[]{:S(2)}) collective-permute-start(f32[3,2,8,128]{3,1,2,0:T(2,128)S(1)} %get-tuple-element.112), channel_id=1, source_target_pairs={{8,0},{16,8},{24,16},{9,1},{17,9},{25,17},{10,2},{18,10},{26,18},{... | collective-permute-start | bytes 73736 | tf_op jit(solution)/shard_map/ppermute | solution.py:23
  74.4 3.9 %collective-permute-start.12 = (f32[3,2,8,128]{3,1,2,0:T(2,128)S(1)}, f32[3,2,8,128]{3,1,2,0:T(2,128)S(1)}, u32[]{:S(2)}, u32[]{:S(2)}) collective-permute-start(f32[3,2,8,128]{3,1,2,0:T(2,128)S(1)} %get-tuple-element.109), channel_id=1, source_target_pairs={{0,8},{8,16},{16,24},{1,9},{9,17},{17,25},{2,10},{10,18},{18,26},{... | collective-permute-start | bytes 73736 | tf_op jit(solution)/shard_map/ppermute | solution.py:20
  77.1 4.6 %collective-permute-start.13 = (f32[3,2,8,128]{3,1,2,0:T(2,128)S(1)}, f32[3,2,8,128]{3,1,2,0:T(2,128)S(1)}, u32[]{:S(2)}, u32[]{:S(2)}) collective-permute-start(f32[3,2,8,128]{3,1,2,0:T(2,128)S(1)} %get-tuple-element.110), channel_id=1, source_target_pairs={{8,0},{16,8},{24,16},{9,1},{17,9},{25,17},{10,2},{18,10},{26,18},{... | collective-permute-start | bytes 73736 | tf_op jit(solution)/shard_map/ppermute | solution.py:23
  81.7 8.4 %collective-permute-start.14 = (f32[3,36,2,128]{3,1,2,0:T(8,128)S(1)}, f32[3,36,2,128]{3,1,2,0:T(8,128)S(1)}, u32[]{:S(2)}, u32[]{:S(2)}) collective-permute-start(f32[3,36,2,128]{3,1,2,0:T(8,128)S(1)} %get-tuple-element.105), channel_id=1, source_target_pairs={{0,1},{1,2},{2,3},{3,4},{4,5},{5,6},{6,7},{8,9},{9,10},{10,11},{11... | collective-permute-start | bytes 331784 | tf_op jit(solution)/shard_map/ppermute | solution.py:20
  87.2 6.2 %collective-permute-start.15 = (f32[3,36,2,128]{3,1,2,0:T(8,128)S(1)}, f32[3,36,2,128]{3,1,2,0:T(8,128)S(1)}, u32[]{:S(2)}, u32[]{:S(2)}) collective-permute-start(f32[3,36,2,128]{3,1,2,0:T(8,128)S(1)} %get-tuple-element.106), channel_id=1, source_target_pairs={{1,0},{2,1},{3,2},{4,3},{5,4},{6,5},{7,6},{9,8},{10,9},{11,10},{12... | collective-permute-start | bytes 331784 | tf_op jit(solution)/shard_map/ppermute | solution.py:23
where the time goes:
time: 109 us; the launch traced here: 108 us
  starting transfers between devices  44.2 us (41%)
  other arithmetic  34.6 us (32%)
  waiting for transfers between devices  17.8 us (16%)
  local copies, waits for them, and re-layouts  9.41 us (9%)
  between operations  1.37 us (1%)
    ppermute x8, starting transfers between devices, extended(): lax.ppermute(lax.slice_in_dim(block, block.shape[dim] - width, None, axis...  30.7 us
    unnamed x20, other arithmetic  23.7 us
    ppermute x8, waiting for transfers between devices, extended(): lax.ppermute(lax.slice_in_dim(block, 0, width, axis=dim), axis, backward)  17.8 us
    ppermute x8, starting transfers between devices, extended(): lax.ppermute(lax.slice_in_dim(block, 0, width, axis=dim), axis, backward)  13.5 us
    concatenate x5, other arithmetic, extended(): block = jnp.concatenate([low, block, high], axis=dim)  5.83 us
    unnamed x31, local copies, waits for them, and re-layouts  3.74 us
    slice x7, local copies, waits for them, and re-layouts, crop(): result = lax.slice_in_dim(result, begin, begin + length, axis=dim)  3.06 us
    another operation x6, other arithmetic, split_velocity_update(): forces = jnp.stack([force_x, force_y, force_z])  2.74 us
  transfers between devices with their start and end apart: 16, of which 6 were waited for; matrix products, arithmetic and copies ran while one was open for 5% of the time, Pallas kernels for 0%

commit v1 on v0

v1 whole, which is shorter than its diff:
```python
import functools

import jax
import jax.numpy as jnp
from jax import lax
from jax.experimental import pallas as pl
from jax.experimental.pallas import tpu as pltpu
from jax.sharding import PartitionSpec as P

STEPS = 2
time_step = 0.1
shear_floor = 0.25
MESH = pl.DeviceIdType.MESH
CH = 8
R = 16
UNROLL = 2

STRESS_X = ((0, 1, 2), (3, 2, 1), (4, 2, 1))
STRESS_Y = ((3, 2, 1), (1, 1, 2), (5, 2, 1))
FLOW_X = ((0, 2, 1), (1, 1, 2), (2, 1, 2))
FLOW_Y = ((0, 1, 2), (1, 2, 1), (2, 1, 2))
SPEC = {"s": (STRESS_X, STRESS_Y), "v": (FLOW_X, FLOW_Y)}


def kernel(
    nx,
    ny,
    vel_hbm, str_hbm, lam_hbm, mod_hbm, buo_hbm, zone_hbm, elig_hbm,
    coh_ref, fri_ref, cell_ref, moment_ref,
    vout_hbm, sout_hbm,
    stage, vel, lam, mod, buo, zone, elig, inj, cc, cf, sout,
    xb, yb, zb, pack_up, pack_dn, recv_up, recv_dn,
    load_sem, store_sem, xsend, xrecv, ysend, yrecv,
):
    rows_x = lam.shape[0]
    rows_y = lam.shape[1]
    depth = lam.shape[2]
    chunks = rows_x // CH
    block = R * (rows_x + 1)
    phases = 2 * STEPS
    ix = lax.axis_index("gx")
    iy = lax.axis_index("gy")
    x_lo, x_hi, y_lo, y_hi = ix > 0, ix < nx - 1, iy > 0, iy < ny - 1

    loads = []

    def load(src, dst):
        copy = pltpu.make_async_copy(src, dst, load_sem.at[len(loads)])
        copy.start()
        loads.append(copy)

    for slot, (comp, _, _) in enumerate(STRESS_X):
        load(str_hbm.at[comp], xb.at[0, slot, pl.ds(2, rows_x)])
    load(str_hbm.at[1], stage.at[0])
    load(str_hbm.at[5], stage.at[1])
    load(str_hbm.at[2], zb.at[0])
    load(zone_hbm, zone)
    load(elig_hbm, elig)
    load(vel_hbm, vel)
    load(buo_hbm, buo)
    load(lam_hbm, lam)
    load(mod_hbm, mod)

    barrier = pltpu.get_barrier_semaphore()
    sides = (
        (x_lo, (ix - 1, iy)),
        (x_hi, (ix + 1, iy)),
        (y_lo, (ix, iy - 1)),
        (y_hi, (ix, iy + 1)),
    )
    for there, target in sides:

        @pl.when(there)
        def _():
            pl.semaphore_signal(barrier, inc=1, device_id=target, device_id_type=MESH)

    zero = jnp.zeros((rows_y, depth), jnp.float32)

    @pl.when(jnp.logical_not(x_lo))
    def _():
        for p in range(phases):
            for slot in range(3):
                for layer in (0, 1):
                    xb[p, slot, layer] = zero

    @pl.when(jnp.logical_not(x_hi))
    def _():
        for p in range(phases):
            for slot in range(3):
                for layer in (rows_x + 2, rows_x + 3):
                    xb[p, slot, layer] = zero

    @pl.when(jnp.logical_not(y_lo))
    def _():
        for p in range(phases):
            for c in range(chunks):
                recv_up[p, c] = jnp.zeros(recv_up.shape[2:], jnp.float32)

    @pl.when(jnp.logical_not(y_hi))
    def _():
        for p in range(phases):
            for c in range(chunks):
                recv_dn[p, c] = jnp.zeros(recv_dn.shape[2:], jnp.float32)

    def x_copy(p, slot, up):
        comp, low, high = SPEC["sv"[p % 2]][0][slot]
        if up:
            src = xb.at[p, slot, pl.ds(rows_x + 2 - low, low)]
            dst = xb.at[p, slot, pl.ds(2 - low, low)]
            target = (ix + 1, iy)
        else:
            src = xb.at[p, slot, pl.ds(2, high)]
            dst = xb.at[p, slot, pl.ds(rows_x + 2, high)]
            target = (ix - 1, iy)
        way = 0 if up else 1
        return pltpu.make_async_remote_copy(
            src_ref=src,
            dst_ref=dst,
            send_sem=xsend.at[p, way, slot],
            recv_sem=xrecv.at[p, way, slot],
            device_id=target,
            device_id_type=MESH,
        )

    def y_layers(p):
        spec = SPEC["sv"[p % 2]][1]
        up = [(slot, rows_y - low + i, i - low) for slot, (_, low, _) in enumerate(spec) for i in range(low)]
        dn = [(slot, i, rows_y + i) for slot, (_, _, high) in enumerate(spec) for i in range(high)]
        return up, dn

    def y_copy(p, c, up):
        rows = CH * len(y_layers(p)[0 if up else 1])
        packed, recv = (pack_up, recv_up) if up else (pack_dn, recv_dn)
        way = 0 if up else 1
        return pltpu.make_async_remote_copy(
            src_ref=packed.at[p, c, pl.ds(0, rows)],
            dst_ref=recv.at[p, c, pl.ds(0, rows)],
            send_sem=ysend.at[p, way, c],
            recv_sem=yrecv.at[p, way, c],
            device_id=(ix, iy + 1) if up else (ix, iy - 1),
            device_id_type=MESH,
        )

    def send_x(p, up):
        @pl.when(x_hi if up else x_lo)
        def _():
            for slot in range(3):
                x_copy(p, slot, up).start()

    def take_x(p, up):
        @pl.when(x_lo if up else x_hi)
        def _():
            for slot in range(3):
                x_copy(p, slot, up).wait_recv()

    def ybase(p, slot, x):
        return (p * 3 + slot) * block + R * (x + 1)

    def send_y(p, c):
        up, dn = y_layers(p)
        for layers, packed in ((up, pack_up), (dn, pack_dn)):
            for i, (slot, row, _) in enumerate(layers):
                start = ybase(p, slot, c * CH) + row
                packed[p, c, pl.ds(i * CH, CH), :] = yb[pl.ds(start, CH, stride=R), :]
        for there, way in ((y_hi, True), (y_lo, False)):

            @pl.when(there)
            def _():
                y_copy(p, c, way).start()

    def take_y(p, c):
        for there, way in ((y_lo, True), (y_hi, False)):

            @pl.when(there)
            def _():
                y_copy(p, c, way).wait_recv()

        up, dn = y_layers(p)
        for layers, recv in ((up, recv_up), (dn, recv_dn)):
            for i, (slot, _, row) in enumerate(layers):
                start = ybase(p, slot, c * CH) + row
                yb[pl.ds(start, CH, stride=R), :] = recv[p, c, pl.ds(i * CH, CH), :]

    order = [0] + ([chunks - 1] if chunks > 1 else []) + list(range(1, chunks - 1))

    for copy in loads[:5]:
        copy.wait()

    def fill_y(c):
        def fill(i, carry):
            x = c * CH + i
            for slot, source in enumerate((None, 0, 1)):
                value = xb[0, 1, x + 2] if source is None else stage[source, x]
                yb[pl.ds(pl.multiple_of(ybase(0, slot, x), 8), rows_y), :] = value
            return carry

        lax.fori_loop(0, CH, fill, 0, unroll=True)

    heard = sum(there.astype(jnp.int32) for there, _ in sides)
    pl.semaphore_wait(barrier, heard)
    send_x(0, True)
    send_x(0, False)
    for c in order:
        fill_y(c)
        send_y(0, c)

    cell = cell_ref[...]
    bits = depth.bit_length() - 1
    assert depth == 1 << bits
    plane_row = cell >> bits
    cell_z = cell & (depth - 1)
    row = lax.broadcasted_iota(jnp.int32, (rows_x * rows_y, cell.shape[1]), 0)
    row_bits = rows_y.bit_length() - 1
    assert rows_y == 1 << row_bits
    row = (ix * rows_x + (row >> row_bits)) * (ny * rows_y) + iy * rows_y + (row & (rows_y - 1))
    match = row == plane_row
    at_z = (lax.broadcasted_iota(jnp.int32, (depth, cell.shape[1]), 0) == cell_z).astype(jnp.float32)
    for comp in range(6):
        moment = time_step * moment_ref[pl.ds(comp, 1), :]
        value = lax.dot_general(
            jnp.where(match, moment, 0.0),
            at_z,
            (((1,), (1,)), ((), ())),
            precision=lax.Precision.HIGHEST,
            preferred_element_type=jnp.float32,
        )
        inj[comp] = value.reshape(rows_x, rows_y, depth)

    for copy in loads[6:8]:
        copy.wait()
    frictions, cohesions = [], []
    for which in range(coh_ref.shape[0]):
        f = jnp.full((rows_y, depth), fri_ref[which], jnp.float32)
        frictions.append(f)
        cohesions.append(coh_ref[which] * jnp.sqrt(1.0 - f * f))

    def table(x, carry):
        z = jnp.where(elig[x] == 1, zone[x], -1)
        c = jnp.full((rows_y, depth), 1e30, jnp.float32)
        f = jnp.zeros((rows_y, depth), jnp.float32)
        for which in range(coh_ref.shape[0]):
            hit = z == which
            c = jnp.where(hit, cohesions[which], c)
            f = jnp.where(hit, frictions[which], f)
        cc[x] = c
        cf[x] = f
        return carry

    lax.fori_loop(0, rows_x, table, 0, unroll=2)

    lane = lax.broadcasted_iota(jnp.int32, (rows_y, depth), 1)
    keep = {
        1: lane < depth - 1,
        2: lane < depth - 2,
        -1: lane >= 1,
        -2: lane >= 2,
    }

    def along_z(value, offset):
        if offset == 0:
            return value
        return jnp.where(keep[offset], pltpu.roll(value, (-offset) % depth, 1), 0.0)

    def derivative(get, forward):
        a, b, c, d = (get(1), get(0), get(2), get(-1)) if forward else (get(0), get(-1), get(1), get(-2))
        return 27.0 * (a - b) - (c - d)

    def dx(p, slot, x, forward):
        return derivative(lambda o: xb[p, slot, x + 2 + o], forward)

    def dy(p, slot, x, forward):
        return derivative(lambda o: yb[pl.ds(ybase(p, slot, x) + o, rows_y), :], forward)

    def dz(value, forward):
        return derivative(lambda o: along_z(value, o), forward)

    def put_y(p, slot, x, value):
        yb[pl.ds(pl.multiple_of(ybase(p, slot, x), 8), rows_y), :] = value

    def own_y(p, slot, x):
        return yb[pl.ds(pl.multiple_of(ybase(p, slot, x), 8), rows_y), :]

    def flow_layer(p, x):
        step = p // 2
        s = p
        scale = (time_step / 24.0) * buo[x]
        xz = xb[s, 2, x + 2]
        yz = own_y(s, 2, x)
        zz = zb[step, x]
        force_x = dx(s, 0, x, True) + dy(s, 0, x, False) + dz(xz, False)
        force_y = dx(s, 1, x, False) + dy(s, 1, x, True) + dz(yz, False)
        force_z = dx(s, 2, x, False) + dy(s, 2, x, False) + dz(zz, True)
        for slot, force in enumerate((force_x, force_y, force_z)):
            old = vel[slot, x] if step == 0 else xb[p - 1, slot, x + 2]
            new = old + scale * force
            xb[p + 1, slot, x + 2] = new
            put_y(p + 1, slot, x, new)

    def stress_layer(p, x):
        step = p // 2
        vx, vy, vz = (xb[p, slot, x + 2] for slot in range(3))
        ex = dx(p, 0, x, False)
        ey = dy(p, 1, x, False)
        ez = dz(vz, False)
        xy = dy(p, 0, x, True) + dx(p, 1, x, True)
        xz = dz(vx, True) + dx(p, 2, x, True)
        yz = dz(vy, True) + dy(p, 2, x, True)
        m = (time_step / 24.0) * mod[x]
        spread = (time_step / 24.0) * lam[x] * (ex + ey + ez)
        m2 = m + m
        s0, s3, s4 = (xb[p - 1, slot, x + 2] for slot in range(3))
        s1, s5 = own_y(p - 1, 1, x), own_y(p - 1, 2, x)
        s2 = zb[step, x]
        s0 = s0 + (spread + m2 * ex) + inj[0, x]
        s1 = s1 + (spread + m2 * ey) + inj[1, x]
        s2 = s2 + (spread + m2 * ez) + inj[2, x]
        s3 = s3 + m * xy + inj[3, x]
        s4 = s4 + m * xz + inj[4, x]
        s5 = s5 + m * yz + inj[5, x]
        pressure = (s0 + s1 + s2) * (1.0 / 3.0)
        d0, d1, d2 = s0 - pressure, s1 - pressure, s2 - pressure
        second = 0.5 * (d0 * d0 + d1 * d1 + d2 * d2) + (s3 * s3 + s4 * s4 + s5 * s5)
        strength = jnp.maximum(cc[x] - pressure * cf[x], 0.0)
        factor = jnp.minimum(1.0, strength * lax.rsqrt(jnp.maximum(second, shear_floor * shear_floor)))
        s0, s1, s2 = pressure + factor * d0, pressure + factor * d1, pressure + factor * d2
        s3, s4, s5 = factor * s3, factor * s4, factor * s5
        if p == phases - 1:
            for comp, value in enumerate((s0, s1, s2, s3, s4, s5)):
                sout[comp, x] = value
            return
        for slot, value in enumerate((s0, s3, s4)):
            xb[p + 1, slot, x + 2] = value
        for slot, value in enumerate((s3, s1, s5)):
            put_y(p + 1, slot, x, value)
        zb[step + 1, x] = s2

    stores = []

    def store(src, dst):
        copy = pltpu.make_async_copy(src, dst, store_sem.at[len(stores)])
        copy.start()
        stores.append(copy)

    waited = {5: False, 8: False, 9: False, 10: False, 11: False}

    def need(*which):
        for i in which:
            if not waited[i]:
                waited[i] = True
                loads[i].wait()

    for p in range(phases):
        if p % 2 == 0:
            need(5, 8, 9)
            layer_of = flow_layer
        else:
            need(10, 11)
            layer_of = stress_layer
        for c in order:
            if c == 0:
                take_x(p, True)
            if c == chunks - 1:
                take_x(p, False)
            take_y(p, c)

            def one(i, carry, p=p, c=c, layer_of=layer_of):
                layer_of(p, c * CH + i)
                return carry

            lax.fori_loop(0, CH, one, 0, unroll=UNROLL)
            span = pl.ds(c * CH, CH)
            if p < phases - 1:
                if c == 0:
                    send_x(p + 1, False)
                if c == chunks - 1:
                    send_x(p + 1, True)
                send_y(p + 1, c)
            else:
                store(sout.at[:, span], sout_hbm.at[:, span])
            if p == phases - 2:
                for slot in range(3):
                    store(xb.at[p + 1, slot, pl.ds(2 + c * CH, CH)], vout_hbm.at[slot, span])

    for p in range(phases):
        for there, way in ((x_hi, True), (x_lo, False)):

            @pl.when(there)
            def _():
                for slot in range(3):
                    x_copy(p, slot, way).wait_send()

        for there, way in ((y_hi, True), (y_lo, False)):

            @pl.when(there)
            def _():
                for c in range(chunks):
                    y_copy(p, c, way).wait_send()

    for copy in stores:
        copy.wait()


def on_device(nx, ny, velocity, stress, lame_first, modulus, buoyancy, zone, eligible, cohesion, friction, source_cell, source_moment):
    rows_x, rows_y, depth = zone.shape
    assert rows_y <= 8 and rows_x % CH == 0
    chunks = rows_x // CH
    phases = 2 * STEPS
    f32 = jnp.float32
    grid = (rows_x, rows_y, depth)
    any_spec = pl.BlockSpec(memory_space=pltpu.HBM)
    smem = pl.BlockSpec(memory_space=pltpu.SMEM)
    vmem = pl.BlockSpec(memory_space=pltpu.VMEM)
    return pl.pallas_call(
        functools.partial(kernel, nx, ny),
        out_shape=(jax.ShapeDtypeStruct((3,) + grid, f32), jax.ShapeDtypeStruct((6,) + grid, f32)),
        in_specs=[any_spec] * 7 + [smem, smem, vmem, vmem],
        out_specs=(any_spec, any_spec),
        scratch_shapes=[
            pltpu.VMEM((2,) + grid, f32),
            pltpu.VMEM((3,) + grid, f32),
            pltpu.VMEM(grid, f32),
            pltpu.VMEM(grid, f32),
            pltpu.VMEM(grid, f32),
            pltpu.VMEM(grid, jnp.int32),
            pltpu.VMEM(grid, jnp.int32),
            pltpu.VMEM((6,) + grid, f32),
            pltpu.VMEM(grid, f32),
            pltpu.VMEM(grid, f32),
            pltpu.VMEM((6,) + grid, f32),
            pltpu.VMEM((phases, 3, rows_x + 4, rows_y, depth), f32),
            pltpu.VMEM((phases * 3 * R * (rows_x + 1) + R, depth), f32),
            pltpu.VMEM((STEPS,) + grid, f32),
            pltpu.VMEM((phases, chunks, 5 * CH, depth), f32),
            pltpu.VMEM((phases, chunks, 5 * CH, depth), f32),
            pltpu.VMEM((phases, chunks, 5 * CH, depth), f32),
            pltpu.VMEM((phases, chunks, 5 * CH, depth), f32),
            pltpu.SemaphoreType.DMA((12,)),
            pltpu.SemaphoreType.DMA((4 * chunks,)),
            pltpu.SemaphoreType.DMA((phases, 2, 3)),
            pltpu.SemaphoreType.DMA((phases, 2, 3)),
            pltpu.SemaphoreType.DMA((phases, 2, chunks)),
            pltpu.SemaphoreType.DMA((phases, 2, chunks)),
        ],
        compiler_params=pltpu.CompilerParams(collective_id=0, has_side_effects=True),
    )(
        velocity, stress, lame_first, modulus, buoyancy, zone, eligible,
        cohesion, friction, source_cell.reshape(1, -1), source_moment,
    )


def solution(mesh):
    field = P(None, "gx", "gy", None)
    cells = P("gx", "gy", None)
    return jax.shard_map(
        functools.partial(on_device, mesh.shape["gx"], mesh.shape["gy"]),
        mesh=mesh,
        in_specs=(field, field, cells, cells, cells, cells, cells, P(), P(), P(), P()),
        out_specs=(field, field),
        check_vma=False,
    )
```

time: 109 us -> 24.1 us (0.22)
  the two profiles are of different devices: /device:TPU:1 before, /device:TPU:21 now
where the time goes in v1:
time: 24.1 us; the launch traced here: 23.9 us
  Pallas kernels  20.5 us (85%)
  local copies, waits for them, and re-layouts  2.72 us (11%)
  between operations  0.65 us (3%)
    pallas_call x1, Pallas kernels, on_device(): pl.pallas_call(functools.partial(kernel, nx, ny), out_shape=(jax.ShapeDty...  20.5 us
    unnamed x4, local copies, waits for them, and re-layouts  2.72 us

profile of v1, /device:TPU:21, one launch (start us, length us, event | category | flops | bytes accessed | tf_op | source)
XLA Modules:
  0.0 23.9 jit_solution(13992996252050535354)
XLA Ops:
  0.6 20.5 %shard_map.122 = (f32[3,32,8,128]{3,2,1,0:T(8,128)}, f32[6,32,8,128]{3,2,1,0:T(8,128)}) custom-call(f32[3,32,8,128]{3,2,1,0:T(8,128)} %vel_hbm.1, f32[6,32,8,128]{3,2,1,0:T(8,128)} %str_hbm.1, f32[32,8,128]{2,1,0:T(8,128)} %lam_hbm.1, f32[32,8,128]{2,1,0:T(8,128)} %mod_hbm.1, f32[32,8,128]{2,1,0:T(8,128)} %buo_hbm.1, s32[32,8,128]{2,1,0:T(8,128)} %zone_hbm.1, ...), custom_call_target="tpu_custom_call" | custom-call | tf_op jit(solution)/shard_map/pallas_call | solution.py:413
  21.2 0.0 copy-start
  21.2 1.8 %copy.15 = f32[3,32,8,128]{3,2,1,0:T(8,128)} copy(f32[3,32,8,128]{3,2,1,0:T(8,128)} %get-tuple-element.4) | data formatting | bytes 786432
  23.0 0.0 copy-done
  23.0 0.9 %copy.16 = f32[6,32,8,128]{3,2,1,0:T(8,128)} copy(f32[6,32,8,128]{3,2,1,0:T(8,128)S(1)} %copy-done) | data formatting | bytes 1572864
Async XLA Ops:
  21.2 1.9 %copy-start = (f32[6,32,8,128]{3,2,1,0:T(8,128)S(1)}, f32[6,32,8,128]{3,2,1,0:T(8,128)}, u32[]{:S(2)}) copy-start(f32[6,32,8,128]{3,2,1,0:T(8,128)} %get-tuple-element.5) | copy-start | bytes 2359300

commit v2 on v1

--- a/solution.py
+++ b/solution.py
@@ -13,7 +13,6 @@
 MESH = pl.DeviceIdType.MESH
 CH = 8
 R = 16
-UNROLL = 2
 
 STRESS_X = ((0, 1, 2), (3, 2, 1), (4, 2, 1))
 STRESS_Y = ((3, 2, 1), (1, 1, 2), (5, 2, 1))
@@ -27,10 +26,10 @@
     ny,
     vel_hbm, str_hbm, lam_hbm, mod_hbm, buo_hbm, zone_hbm, elig_hbm,
     coh_ref, fri_ref, cell_ref, moment_ref,
-    vout_hbm, sout_hbm,
-    stage, vel, lam, mod, buo, zone, elig, inj, cc, cf, sout,
+    vout_ref, sout_ref,
+    xe, stage, vel, lam, mod, buo, zone, elig, inj, cc, cf,
     xb, yb, zb, pack_up, pack_dn, recv_up, recv_dn,
-    load_sem, store_sem, xsend, xrecv, ysend, yrecv,
+    load_sem, xsend, xrecv, ysend, yrecv,
 ):
     rows_x = lam.shape[0]
     rows_y = lam.shape[1]
@@ -42,25 +41,6 @@
     iy = lax.axis_index("gy")
     x_lo, x_hi, y_lo, y_hi = ix > 0, ix < nx - 1, iy > 0, iy < ny - 1
 
-    loads = []
-
-    def load(src, dst):
-        copy = pltpu.make_async_copy(src, dst, load_sem.at[len(loads)])
-        copy.start()
-        loads.append(copy)
-
-    for slot, (comp, _, _) in enumerate(STRESS_X):
-        load(str_hbm.at[comp], xb.at[0, slot, pl.ds(2, rows_x)])
-    load(str_hbm.at[1], stage.at[0])
-    load(str_hbm.at[5], stage.at[1])
-    load(str_hbm.at[2], zb.at[0])
-    load(zone_hbm, zone)
-    load(elig_hbm, elig)
-    load(vel_hbm, vel)
-    load(buo_hbm, buo)
-    load(lam_hbm, lam)
-    load(mod_hbm, mod)
-
     barrier = pltpu.get_barrier_semaphore()
     sides = (
         (x_lo, (ix - 1, iy)),
@@ -74,6 +54,31 @@
         def _():
             pl.semaphore_signal(barrier, inc=1, device_id=target, device_id_type=MESH)
 
+    loads = []
+
+    def load(src, dst):
+        copy = pltpu.make_async_copy(src, dst, load_sem.at[len(loads)])
+        copy.start()
+        loads.append(copy)
+
+    for slot, (comp, low, high) in enumerate(STRESS_X):
+        load(str_hbm.at[comp, pl.ds(rows_x - low, low)], xe.at[0, slot, pl.ds(0, low)])
+        load(str_hbm.at[comp, pl.ds(0, high)], xe.at[1, slot, pl.ds(0, high)])
+    edges, rest = len(loads), len(loads) + 3
+    load(str_hbm.at[3], xb.at[0, 1, pl.ds(2, rows_x)])
+    load(str_hbm.at[1], stage.at[0])
+    load(str_hbm.at[5], stage.at[1])
+    load(zone_hbm, zone)
+    load(elig_hbm, elig)
+    load(str_hbm.at[0], xb.at[0, 0, pl.ds(2, rows_x)])
+    load(str_hbm.at[4], xb.at[0, 2, pl.ds(2, rows_x)])
+    load(str_hbm.at[2], zb.at[0])
+    load(vel_hbm, vel)
+    load(buo_hbm, buo)
+    late = len(loads)
+    load(lam_hbm, lam)
+    load(mod_hbm, mod)
+
     zero = jnp.zeros((rows_y, depth), jnp.float32)
 
     @pl.when(jnp.logical_not(x_lo))
@@ -105,11 +110,11 @@
     def x_copy(p, slot, up):
         comp, low, high = SPEC["sv"[p % 2]][0][slot]
         if up:
-            src = xb.at[p, slot, pl.ds(rows_x + 2 - low, low)]
+            src = xe.at[0, slot, pl.ds(0, low)] if p == 0 else xb.at[p, slot, pl.ds(rows_x + 2 - low, low)]
             dst = xb.at[p, slot, pl.ds(2 - low, low)]
             target = (ix + 1, iy)
         else:
-            src = xb.at[p, slot, pl.ds(2, high)]
+            src = xe.at[1, slot, pl.ds(0, high)] if p == 0 else xb.at[p, slot, pl.ds(2, high)]
             dst = xb.at[p, slot, pl.ds(rows_x + 2, high)]
             target = (ix - 1, iy)
         way = 0 if up else 1
@@ -183,7 +188,7 @@
 
     order = [0] + ([chunks - 1] if chunks > 1 else []) + list(range(1, chunks - 1))
 
-    for copy in loads[:5]:
+    for copy in loads[:edges]:
         copy.wait()
 
     def fill_y(c):
@@ -200,6 +205,8 @@
     pl.semaphore_wait(barrier, heard)
     send_x(0, True)
     send_x(0, False)
+    for copy in loads[edges:rest]:
+        copy.wait()
     for c in order:
         fill_y(c)
         send_y(0, c)
@@ -226,7 +233,7 @@
         )
         inj[comp] = value.reshape(rows_x, rows_y, depth)
 
-    for copy in loads[6:8]:
+    for copy in loads[rest : rest + 2]:
         copy.wait()
     frictions, cohesions = [], []
     for which in range(coh_ref.shape[0]):
@@ -295,6 +302,8 @@
             new = old + scale * force
             xb[p + 1, slot, x + 2] = new
             put_y(p + 1, slot, x, new)
+            if p == phases - 2:
+                vout_ref[slot, x] = new
 
     def stress_layer(p, x):
         step = p // 2
@@ -326,7 +335,7 @@
         s3, s4, s5 = factor * s3, factor * s4, factor * s5
         if p == phases - 1:
             for comp, value in enumerate((s0, s1, s2, s3, s4, s5)):
-                sout[comp, x] = value
+                sout_ref[comp, x] = value
             return
         for slot, value in enumerate((s0, s3, s4)):
             xb[p + 1, slot, x + 2] = value
@@ -334,28 +343,14 @@
             put_y(p + 1, slot, x, value)
         zb[step + 1, x] = s2
 
-    stores = []
-
-    def store(src, dst):
-        copy = pltpu.make_async_copy(src, dst, store_sem.at[len(stores)])
-        copy.start()
-        stores.append(copy)
-
-    waited = {5: False, 8: False, 9: False, 10: False, 11: False}
-
-    def need(*which):
-        for i in which:
-            if not waited[i]:
-                waited[i] = True
-                loads[i].wait()
-
     for p in range(phases):
-        if p % 2 == 0:
-            need(5, 8, 9)
-            layer_of = flow_layer
-        else:
-            need(10, 11)
-            layer_of = stress_layer
+        layer_of = flow_layer if p % 2 == 0 else stress_layer
+        if p == 0:
+            for copy in loads[rest + 2 : late]:
+                copy.wait()
+        elif p == 1:
+            for copy in loads[late:]:
+                copy.wait()
         for c in order:
             if c == 0:
                 take_x(p, True)
@@ -367,19 +362,13 @@
                 layer_of(p, c * CH + i)
                 return carry
 
-            lax.fori_loop(0, CH, one, 0, unroll=UNROLL)
-            span = pl.ds(c * CH, CH)
+            lax.fori_loop(0, CH, one, 0, unroll=True)
             if p < phases - 1:
                 if c == 0:
                     send_x(p + 1, False)
                 if c == chunks - 1:
                     send_x(p + 1, True)
                 send_y(p + 1, c)
-            else:
-                store(sout.at[:, span], sout_hbm.at[:, span])
-            if p == phases - 2:
-                for slot in range(3):
-                    store(xb.at[p + 1, slot, pl.ds(2 + c * CH, CH)], vout_hbm.at[slot, span])
 
     for p in range(phases):
         for there, way in ((x_hi, True), (x_lo, False)):
@@ -395,9 +384,6 @@
             def _():
                 for c in range(chunks):
                     y_copy(p, c, way).wait_send()
-
-    for copy in stores:
-        copy.wait()
 
 
 def on_device(nx, ny, velocity, stress, lame_first, modulus, buoyancy, zone, eligible, cohesion, friction, source_cell, source_moment):
@@ -412,10 +398,11 @@
     vmem = pl.BlockSpec(memory_space=pltpu.VMEM)
     return pl.pallas_call(
         functools.partial(kernel, nx, ny),
-        out_shape=(jax.ShapeDtypeStruct((3,) + grid, f32), jax.ShapeDtypeStruct((6,) + grid, f32)),
+        out_shape=(pltpu.VMEM((3,) + grid, f32), pltpu.VMEM((6,) + grid, f32)),
         in_specs=[any_spec] * 7 + [smem, smem, vmem, vmem],
-        out_specs=(any_spec, any_spec),
+        out_specs=(vmem, vmem),
         scratch_shapes=[
+            pltpu.VMEM((2, 3, 2, rows_y, depth), f32),
             pltpu.VMEM((2,) + grid, f32),
             pltpu.VMEM((3,) + grid, f32),
             pltpu.VMEM(grid, f32),
@@ -426,7 +413,6 @@
             pltpu.VMEM((6,) + grid, f32),
             pltpu.VMEM(grid, f32),
             pltpu.VMEM(grid, f32),
-            pltpu.VMEM((6,) + grid, f32),
             pltpu.VMEM((phases, 3, rows_x + 4, rows_y, depth), f32),
             pltpu.VMEM((phases * 3 * R * (rows_x + 1) + R, depth), f32),
             pltpu.VMEM((STEPS,) + grid, f32),
@@ -434,8 +420,7 @@
             pltpu.VMEM((phases, chunks, 5 * CH, depth), f32),
             pltpu.VMEM((phases, chunks, 5 * CH, depth), f32),
             pltpu.VMEM((phases, chunks, 5 * CH, depth), f32),
-            pltpu.SemaphoreType.DMA((12,)),
-            pltpu.SemaphoreType.DMA((4 * chunks,)),
+            pltpu.SemaphoreType.DMA((18,)),
             pltpu.SemaphoreType.DMA((phases, 2, 3)),
             pltpu.SemaphoreType.DMA((phases, 2, 3)),
             pltpu.SemaphoreType.DMA((phases, 2, chunks)),

time: 24.1 us -> 20.4 us (0.85)
  Pallas kernels: 20.5 us -> 17.9 us
  local copies, waits for them, and re-layouts: 2.72 us -> 1.63 us
    pallas_call x1, Pallas kernels: 20.5 us -> 17.9 us  [on_device(): pl.pallas_call(functools.partial(kernel, nx, ny), out_shape=(pltpu.VMEM((...]
    unnamed x4 -> x2, local copies, waits for them, and re-layouts: 2.72 us -> 1.63 us
where the time goes in v2:
time: 20.4 us; the launch traced here: 20.2 us
  Pallas kernels  17.9 us (88%)
  local copies, waits for them, and re-layouts  1.63 us (8%)
  between operations  0.64 us (3%)
    pallas_call x1, Pallas kernels, on_device(): pl.pallas_call(functools.partial(kernel, nx, ny), out_shape=(pltpu.VMEM((...  17.9 us
    unnamed x2, local copies, waits for them, and re-layouts  1.63 us

profile of v2, /device:TPU:21, one launch (start us, length us, event | category | flops | bytes accessed | tf_op | source)
XLA Modules:
  0.0 20.2 jit_solution(13629314534404950469)
XLA Ops:
  0.6 17.9 %shard_map.122 = (f32[3,32,8,128]{3,2,1,0:T(8,128)S(1)}, f32[6,32,8,128]{3,2,1,0:T(8,128)S(1)}) custom-call(f32[3,32,8,128]{3,2,1,0:T(8,128)} %vel_hbm.1, f32[6,32,8,128]{3,2,1,0:T(8,128)} %str_hbm.1, f32[32,8,128]{2,1,0:T(8,128)} %lam_hbm.1, f32[32,8,128]{2,1,0:T(8,128)} %mod_hbm.1, f32[32,8,128]{2,1,0:T(8,128)} %buo_hbm.1, s32[32,8,128]{2,1,0:T(8,128)} %zone_hbm.1, ...), custom_call_target="tpu_custom_call" | custom-call | tf_op jit(solution)/shard_map/pallas_call | solution.py:399
  18.5 0.7 %copy.15 = f32[3,32,8,128]{3,2,1,0:T(8,128)} copy(f32[3,32,8,128]{3,2,1,0:T(8,128)S(1)} %get-tuple-element.2) | data formatting | bytes 786432
  19.3 0.9 %copy.16 = f32[6,32,8,128]{3,2,1,0:T(8,128)} copy(f32[6,32,8,128]{3,2,1,0:T(8,128)S(1)} %get-tuple-element.3) | data formatting | bytes 1572864
